TPU v7x, 256 devices: a whole 4x4x8 slice. The times are simulated.
256 devices in a mesh: pair: 128 (over x_hi, z, y, core), ao: 2 (over x_lo).
Axes of the slice: x: 4 (x_hi: 2, x_lo: 2; x = x_hi * 2 + x_lo), y: 4, z: 8, core: 2. Of those that a mesh axis runs over, the one named last changes fastest.
Arguments:
- gamma: bfloat16 [128, 1792, 1792], P('pair', 'ao'), may hold values from -6 to 6
- c_vir: bfloat16 [1024, 1792], replicated, may hold values from -0.125 to 0.125
- c_occ: bfloat16 [1024, 256], replicated, may hold values from -1.796875 to 1.796875
- pair_list: int32 [128, 2], replicated, may hold values from 0 to 255
- shell_order: int32 [128], replicated, may hold values from 0 to 127, each once
Outputs:
- ao_density: bfloat16 [1024, 1024], P('ao', 'pair')
Inputs may be any that keep to these rules, and one draw needn't show every extreme that they name: shell_order holds each of 0 to 127 once.
All inputs are finite; a program needn't handle non-finite values.
Results may differ from a plain program's by a relative error of at most 0.0049.
Values sent between devices are 32-bit elements; how exact they have to be, the bound alone decides.
No kernel may reach another device: no remote copies, remote signals or barrier semaphores. Data moves between devices by JAX's collectives and lax.ppermute only.
A program may use at most 64 MiB of HBM per device.

v0:
```python
import jax
import jax.numpy as jnp
from jax import lax
from jax.sharding import PartitionSpec as P

SB = 8


def cut_along(x, dim, length):
    dims = x.shape
    tiles = x.reshape(*dims[:dim], length, dims[dim] // length, *dims[dim + 1 :])
    return jnp.moveaxis(tiles, dim, 0)


def sent_and_summed(x, axis, dim):
    length = lax.axis_size(axis)
    tiles = lax.all_to_all(cut_along(x, dim, length), axis, 0, 0, tiled=True)
    return jnp.sum(tiles, axis=0)


def shards(gamma, c_vir, c_occ, pair_list, shell_order):
    basis = c_vir.shape[0]
    groups = lax.axis_size("pair")
    own_index = lax.axis_index("pair")
    ao_index = lax.axis_index("ao")
    ao_count = lax.axis_size("ao")
    amplitude = gamma[0]
    local_vir = amplitude.shape[0]
    offsets = jnp.arange(SB, dtype=jnp.int32)
    row_index = (shell_order[:, None] * SB + offsets[None, :]).reshape(-1)
    vir_sorted = lax.dynamic_slice_in_dim(c_vir[row_index], ao_index * local_vir, local_vir, 1)
    half_block = lax.dot_general(
        amplitude, c_vir, (((1,), (1,)), ((), ())), preferred_element_type=jnp.float32
    ).astype(jnp.bfloat16)
    owned = basis // groups
    width_nu = basis // ao_count
    my_rows = lax.dynamic_slice_in_dim(row_index, own_index * owned, owned)
    nu_rows = ao_index * width_nu + jnp.arange(width_nu, dtype=jnp.int32)
    summed = sent_and_summed(
        lax.dot_general(
            half_block, vir_sorted, (((0,), (1,)), ((), ())), preferred_element_type=jnp.float32
        ),
        "ao",
        0,
    )
    blocks = lax.all_to_all(summed, "pair", split_axis=1, concat_axis=1, tiled=True)
    values = blocks.reshape(width_nu, groups, owned)
    left_weight = c_occ[my_rows][:, pair_list[:, 0]].astype(jnp.float32)
    right_weight = c_occ[nu_rows][:, pair_list[:, 1]].astype(jnp.float32)
    result = jnp.einsum("np,npr,rp->nr", right_weight, values, left_weight)
    return result.astype(jnp.bfloat16)


def solution(mesh):
    return jax.shard_map(
        shards,
        mesh=mesh,
        in_specs=(P("pair", "ao", None), P(), P(), P(), P()),
        out_specs=P("ao", "pair"),
        check_vma=False,
    )
```

profile of v0, /device:TPU:1, one launch (start us, length us, event | category | flops | bytes accessed | tf_op | source)
XLA Modules:
  0.0 158.2 jit_solution(15369253426494974241)
XLA Ops:
  0.0 0.0 copy-start
  0.0 0.8 broadcast_multiply_fusion
  0.8 0.1 iota_add_fusion
  0.9 0.1 add.91
  1.0 10.4 %gather_fusion.2 = bf16[1024,1792]{1,0:T(8,128)(2,1)} fusion(bf16[1024,1792]{1,0:T(8,128)(2,1)} %param.6, s32[1024]{0:T(1024)S(1)} %broadcast_clamp_fusion), kind=kCustom, calls=%fused_computation.2 | custom fusion | bytes 7344128 | tf_op jit(solution)/shard_map/gather | solution.py:31
  11.5 0.0 copy-done
  11.5 10.2 %fusion.5 = f32[1024,1024]{1,0:T(8,128)} fusion(bf16[1024,1792]{1,0:T(8,128)(2,1)} %gather_fusion.2, s32[]{:T(128)S(6)} %select_n.40, bf16[1024,1792]{1,0:T(8,128)(2,1)} %param.6, bf16[1,896,1792]{2,1,0:T(8,128)(2,1)S(1)} %copy-done), kind=kOutput, calls=%fused_computation.11 | convolution fusion | flops 5168300032 | bytes 12910596 | tf_op jit(solution)/shard_map/dot_general | solution.py:40
  21.7 52.8 %all_to_all.14 = f32[2,512,1024]{2,1,0:T(8,128)} all-to-all(f32[2,512,1024]{2,1,0:T(8,128)} %bitcast.35), channel_id=1, replica_groups=mesh['pair'=128,'ao'=2] {'ao'}, dimensions={0} | all-to-all | bytes 8388608 | tf_op jit(solution)/shard_map/all_to_all | solution.py:17
  74.5 4.1 %reduce_sum.9 = f32[512,1024]{1,0:T(8,128)} reduce(f32[2,512,1024]{2,1,0:T(8,128)} %all_to_all.14, f32[]{:T(128)} %constant.18.clone.1), dimensions={0}, to_apply=%region_0.0 | reduce | flops 524288 | bytes 6291460 | tf_op jit(solution)/shard_map/reduce_sum | solution.py:18
  78.6 2.9 %copy.11 = f32[512,1024]{0,1:T(8,128)} copy(f32[512,1024]{1,0:T(8,128)} %reduce_sum.9) | data formatting | bytes 4194304 | tf_op jit(solution)/shard_map/reduce_sum | solution.py:18
  81.5 0.0 copy-start.1
  81.5 19.2 %all-to-all-start.1 = ((f32[512,128,8]{0,2,1:T(8,128)}), f32[512,128,8]{0,2,1:T(8,128)}, u32[]{:S(2)}, u32[]{:S(2)}) async-start(f32[512,128,8]{0,2,1:T(8,128)} %bitcast.34), calls=%async_computation.1 | async-start | bytes 4194304 | tf_op jit(solution)/shard_map/all_to_all | solution.py:46
  100.7 0.1 add.95
  100.8 0.1 compare_select_fusion.3
  100.9 1.7 %gather_fusion.3 = bf16[8,256]{1,0:T(8,128)(2,1)S(1)} fusion(bf16[1024,256]{1,0:T(8,128)(2,1)} %param.7, s32[1024]{0:T(1024)S(1)} %pad_clamp_fusion.1), kind=kCustom, calls=%fused_computation.3 | custom fusion | bytes 8224 | tf_op jit(solution)/shard_map/gather | solution.py:48
  102.6 0.1 copy.12
  102.7 3.3 %gather_fusion = bf16[512,256]{1,0:T(8,128)(2,1)} fusion(bf16[1024,256]{1,0:T(8,128)(2,1)} %param.7, s32[1024]{0:T(1024)S(1)} %pad_clamp_fusion.3), kind=kCustom, calls=%fused_computation | custom fusion | bytes 526336 | tf_op jit(solution)/shard_map/gather | solution.py:49
  106.0 1.1 copy.10
  107.1 0.0 copy-done.1
  107.2 1.3 gather_fusion.4
  108.5 1.5 gather_fusion.1
  110.0 0.8 convert_bitcast_fusion
  110.7 0.9 bitcast_convert_fusion
  111.7 44.1 %all-to-all-done.1 = f32[512,128,8]{0,2,1:T(8,128)} async-done(((f32[512,128,8]{0,2,1:T(8,128)}), f32[512,128,8]{0,2,1:T(8,128)}, u32[]{:S(2)}, u32[]{:S(2)}) %all-to-all-start.1) | async-done | bytes 2097184 | tf_op jit(solution)/shard_map/all_to_all | solution.py:46
  155.7 2.5 %fusion.4 = bf16[512,8]{0,1:T(8,128)(2,1)} fusion(f32[512,128,8]{0,2,1:T(8,128)} %all-to-all-done.1, f32[512,128]{0,1:T(8,128)S(1)} %bitcast_convert_fusion, f32[8,128]{0,1:T(8,128)S(1)} %convert_bitcast_fusion), kind=kLoop, calls=%fused_computation.10 | loop fusion | flops 1568768 | bytes 2371584 | tf_op jit(solution)/shard_map/np,npr,rp->nr/dot_general | solution.py:50
  (7 shorter events, 0.0 us)
Async XLA Ops:
  0.0 11.5 %copy-start = (bf16[1,896,1792]{2,1,0:T(8,128)(2,1)S(1)}, bf16[1,896,1792]{2,1,0:T(8,128)(2,1)}, u32[]{:S(2)}) copy-start(bf16[1,896,1792]{2,1,0:T(8,128)(2,1)} %param.5) | copy-start | bytes 9633796
  81.5 25.6 %copy-start.1 = (s32[128,2]{0,1:T(2,128)S(1)}, s32[128,2]{0,1:T(2,128)}, u32[]{:S(2)}) copy-start(s32[128,2]{0,1:T(2,128)} %param.8) | copy-start | bytes 3076
  81.5 74.2 %all-to-all-start.1 = ((f32[512,128,8]{0,2,1:T(8,128)}), f32[512,128,8]{0,2,1:T(8,128)}, u32[]{:S(2)}, u32[]{:S(2)}) async-start(f32[512,128,8]{0,2,1:T(8,128)} %bitcast.34), calls=%async_computation.1 | async-start | bytes 4194304 | tf_op jit(solution)/shard_map/all_to_all | solution.py:46
where the time goes:
time: 159 us; the launch traced here: 158 us
  blocking collectives  52.8 us (33%)
  waiting for transfers between devices  44.1 us (28%)
  local copies, waits for them, and re-layouts  22.6 us (14%)
  starting transfers between devices  19.2 us (12%)
  matrix products  10.2 us (6%)
  other arithmetic  9.26 us (6%)
    all_to_all x1, blocking collectives, sent_and_summed(): tiles = lax.all_to_all(cut_along(x, dim, length), axis, 0, 0, tiled=True)  52.8 us
    all_to_all x1, waiting for transfers between devices, shards(): lax.all_to_all(summed, 'pair', split_axis=1, concat_axis=1, tiled=True)  44.1 us
    all_to_all x1, starting transfers between devices, shards(): lax.all_to_all(summed, 'pair', split_axis=1, concat_axis=1, tiled=True)  19.2 us
    gather x1, local copies, waits for them, and re-layouts, shards(): c_vir[row_index]  10.4 us
    dot_general x1, matrix products, shards(): lax.dot_general(half_block, vir_sorted, (((0,), (1,)), ((), ())), preferr...  10.2 us
    gather x3, local copies, waits for them, and re-layouts, shards(): right_weight = c_occ[nu_rows][:, pair_list[:, 1]].astype(jnp.float32)  5.89 us
    reduce_sum x1, other arithmetic, sent_and_summed(): return jnp.sum(tiles, axis=0)  4.09 us
  transfers between devices with their start and end apart: 1, of which 1 were waited for; matrix products, arithmetic and copies ran while one was open for 7% of the time, Pallas kernels for 0%

commit v1 on v0

v1 whole, which is shorter than its diff:
```python
import functools

import jax
import jax.numpy as jnp
from jax import lax
from jax.experimental import pallas as pl
from jax.experimental.pallas import tpu as pltpu
from jax.sharding import Mesh, PartitionSpec as P

SB = 8
TILE = 256
AXES = ("xh", "z", "y", "core", "xl")
NT = (((1,), (1,)), ((), ()))


def amplitude_kernel(where_ref, order_ref, pairs_ref, gamma_hbm, vir_hbm, occ_ref,
                     keep_hbm, send_hbm, gamma, vir, half, left, right, units, slot,
                     gamma_sem, vir_sem, out_sem):
    shells = order_ref.shape[0]
    rows_a = gamma.shape[0]
    step_a = rows_a // 4
    nu_tiles = vir.shape[0] // TILE

    def load_gamma(i):
        part = pl.ds(i * step_a, step_a)
        return pltpu.make_async_copy(gamma_hbm.at[part], gamma.at[part], gamma_sem.at[i])

    def load_vir(j):
        part = pl.ds(j * TILE, TILE)
        return pltpu.make_async_copy(vir_hbm.at[part], vir.at[part], vir_sem.at[j])

    load_vir(0).start()
    for i in range(4):
        load_gamma(i).start()
    for j in range(1, nu_tiles):
        load_vir(j).start()

    my_pair, my_ao, my_core = where_ref[0], where_ref[1], where_ref[2]

    def place(k, _):
        core = k % 2
        y = (k // 2) % 4
        z = (k // 8) % 8
        x = (k // 64) * 2
        x_first = (x * 4 + y) * 8 + z
        y_first = (y * 4 + x) * 8 + z
        base = jnp.where(core == my_core, 0, shells) + jnp.where(core == 0, x_first, y_first)
        shell = order_ref[k]
        slot[0, shell] = base
        slot[1, shell] = base + jnp.where(core == 0, 32, 8)
        return _

    lax.fori_loop(0, shells, place, 0, unroll=4)

    occ = occ_ref[...]
    occupied = occ.shape[1]
    pick_i = lax.broadcasted_iota(jnp.int32, (occupied, 128), 0) == pairs_ref[0, my_pair]
    left[...] = jnp.dot(occ, pick_i.astype(jnp.bfloat16), preferred_element_type=jnp.float32)
    pick_j = lax.broadcasted_iota(jnp.int32, (SB, occupied), 1) == pairs_ref[1, my_pair]
    right[...] = lax.dot_general(pick_j.astype(jnp.bfloat16), occ, NT, preferred_element_type=jnp.float32)

    local = pl.ds(pl.multiple_of(my_ao * rows_a, 128), rows_a)
    load_vir(0).wait()
    for j in range(nu_tiles):
        nu = pl.ds(j * TILE, TILE)
        if j == 0:
            for i in range(4):
                load_gamma(i).wait()
                part = pl.ds(i * step_a, step_a)
                half[part] = lax.dot_general(
                    gamma[part], vir[nu], NT, preferred_element_type=jnp.float32
                ).astype(jnp.bfloat16)
            for t in range(1, nu_tiles):
                load_vir(t).wait()
        else:
            half[...] = lax.dot_general(
                gamma[...], vir[nu], NT, preferred_element_type=jnp.float32
            ).astype(jnp.bfloat16)
        block = jnp.dot(vir[:, local], half[...], preferred_element_type=jnp.float32)
        weight = right[:, nu]
        columns = pl.ds((j % 2) * TILE, TILE)
        for s in range(shells):
            rows = slice(s * SB, (s + 1) * SB)
            scale = left[rows]
            units[slot[j // 2, s], :, columns] = (
                block[rows] * jnp.concatenate([scale, scale], axis=1) * weight
            )
    copies = [
        pltpu.make_async_copy(units.at[pl.ds(shells, shells)], send_hbm, out_sem.at[0]),
        pltpu.make_async_copy(units.at[pl.ds(0, shells)], keep_hbm, out_sem.at[1]),
    ]
    for copy in copies:
        copy.start()
    for copy in copies:
        copy.wait()


def weighted_blocks(where, order, pairs, gamma, vir, occ):
    basis, orbitals = vir.shape
    rows_a = gamma.shape[0]
    shells = order.shape[0]
    width = basis // 2
    out = jax.ShapeDtypeStruct((shells, SB, width), jnp.float32)
    smem = pl.BlockSpec(memory_space=pltpu.SMEM)
    hbm = pl.BlockSpec(memory_space=pl.ANY)
    return pl.pallas_call(
        amplitude_kernel,
        out_shape=(out, out),
        in_specs=[smem, smem, smem, hbm, hbm, pl.BlockSpec(memory_space=pltpu.VMEM)],
        out_specs=(hbm, hbm),
        scratch_shapes=[
            pltpu.VMEM((rows_a, orbitals), jnp.bfloat16),
            pltpu.VMEM((basis, orbitals), jnp.bfloat16),
            pltpu.VMEM((rows_a, TILE), jnp.bfloat16),
            pltpu.VMEM((basis, 128), jnp.float32),
            pltpu.VMEM((SB, basis), jnp.float32),
            pltpu.VMEM((2 * shells, SB, width), jnp.float32),
            pltpu.SMEM((2, shells), jnp.int32),
            pltpu.SemaphoreType.DMA((4,)),
            pltpu.SemaphoreType.DMA((basis // TILE,)),
            pltpu.SemaphoreType.DMA((2,)),
        ],
        compiler_params=pltpu.CompilerParams(vmem_limit_bytes=40 * 2**20),
        cost_estimate=pl.CostEstimate(
            flops=2 * rows_a * basis * (orbitals + basis),
            bytes_accessed=2 * (rows_a + basis) * orbitals + 4 * basis * basis,
            transcendentals=0,
        ),
        name="weighted_blocks",
    )(where, order, pairs, gamma, vir, occ)


def device(x, y, z, core):
    return ((((x // 2) * 8 + z) * 4 + y) * 2 + core) * 2 + x % 2


def shifted(step, ways):
    moves = []
    for x in range(4):
        for y in range(4):
            for z in range(8):
                for core in range(2):
                    to = {"x": x, "y": y, "z": z}
                    name = ways[core]
                    to[name] = (to[name] + step) % (8 if name == "z" else 4)
                    moves.append((device(x, y, z, core), device(core=core, **to)))
    return moves


def exchanged(value, ways, steps):
    count = value.shape[0]
    name = {"x": 2 * lax.axis_index("xh") + lax.axis_index("xl"), "y": lax.axis_index("y"), "z": lax.axis_index("z")}
    core = lax.axis_index("core")
    here = jnp.where(core == 0, name[ways[0]], name[ways[1]])
    total = lax.dynamic_index_in_dim(value, here, 0, keepdims=False)
    for step in steps:
        part = lax.dynamic_index_in_dim(value, (here + step) % count, 0, keepdims=False)
        total = total + lax.ppermute(part, AXES, shifted(step, ways))
    return total


def shards(gamma, c_vir, c_occ, pair_list, shell_order):
    own_pair = lax.axis_index(("xh", "z", "y", "core"))
    where = jnp.stack([own_pair, lax.axis_index("xl"), lax.axis_index("core")]).astype(jnp.int32)
    keep, send = weighted_blocks(where, shell_order, pair_list.T, gamma[0], c_vir, c_occ)
    total = keep + lax.ppermute(send, "core", [(0, 1), (1, 0)])
    total = total.reshape(4, 32, *total.shape[1:])
    total = exchanged(total, ("x", "y"), (1, 3, 2))
    total = total.reshape(4, 8, *total.shape[1:])
    total = exchanged(total, ("y", "x"), (1, 3, 2))
    total = jnp.sum(lax.all_to_all(total, "z", 0, 0, tiled=True), axis=0)
    return total.T.astype(jnp.bfloat16)


def solution(mesh):
    inner = Mesh(mesh.devices.reshape(2, 8, 4, 2, 2), AXES)
    pair = ("xh", "z", "y", "core")
    return jax.shard_map(
        shards,
        mesh=inner,
        in_specs=(P(pair, "xl", None), P(), P(), P(), P()),
        out_specs=P("xl", pair),
        check_vma=False,
    )
```

time: 159 us -> 77.8 us (0.49)
  the two profiles are of different devices: /device:TPU:1 before, /device:TPU:2 now
where the time goes in v1:
time: 77.8 us; the launch traced here: 77.4 us
  waiting for transfers between devices  21.8 us (28%)
  blocking collectives  17.3 us (22%)
  Pallas kernels  16.6 us (21%)
  starting transfers between devices  9.64 us (12%)
  local copies, waits for them, and re-layouts  7.8 us (10%)
  other arithmetic  4.05 us (5%)
    ppermute x6, waiting for transfers between devices, exchanged(): total = total + lax.ppermute(part, AXES, shifted(step, ways))  17.4 us
    all_to_all x1, blocking collectives, shards(): total = jnp.sum(lax.all_to_all(total, 'z', 0, 0, tiled=True), axis=0)  17.3 us
    pallas_call x1, Pallas kernels, weighted_blocks(): pl.pallas_call(amplitude_kernel, out_shape=(out, out), in_specs=[smem, sm...  16.6 us
    ppermute x6, starting transfers between devices, exchanged(): total = total + lax.ppermute(part, AXES, shifted(step, ways))  9.55 us
    unnamed x12, local copies, waits for them, and re-layouts  7.64 us
    ppermute x1, waiting for transfers between devices, shards(): total = keep + lax.ppermute(send, 'core', [(0, 1), (1, 0)])  4.43 us
    add x1, other arithmetic, shards(): total = keep + lax.ppermute(send, 'core', [(0, 1), (1, 0)])  2.07 us
  transfers between devices with their start and end apart: 7, of which 7 were waited for; matrix products, arithmetic and copies ran while one was open for 0% of the time, Pallas kernels for 0%

profile of v1, /device:TPU:2, one launch (start us, length us, event | category | flops | bytes accessed | tf_op | source)
XLA Modules:
  0.0 77.4 jit_solution(10995573928699724963)
XLA Ops:
  0.0 0.1 pad_add_fusion.where_ref
  0.1 0.0 copy-start
  0.1 2.0 %copy-done = bf16[1024,1792]{1,0:T(8,128)(2,1)S(1)} copy-done((bf16[1024,1792]{1,0:T(8,128)(2,1)S(1)}, bf16[1024,1792]{1,0:T(8,128)(2,1)}, u32[]{:S(2)}) %copy-start) | copy-done | bytes 3670040
  2.1 0.0 copy-start.1
  2.1 1.9 %copy-done.1 = bf16[1,896,1792]{2,1,0:T(8,128)(2,1)S(1)} copy-done((bf16[1,896,1792]{2,1,0:T(8,128)(2,1)S(1)}, bf16[1,896,1792]{2,1,0:T(8,128)(2,1)}, u32[]{:S(2)}) %copy-start.1) | copy-done | bytes 3211288
  4.0 0.0 copy-start.2
  4.0 1.0 %copy-done.2 = bf16[1024,256]{1,0:T(8,128)(2,1)S(1)} copy-done((bf16[1024,256]{1,0:T(8,128)(2,1)S(1)}, bf16[1024,256]{1,0:T(8,128)(2,1)}, u32[]{:S(2)}) %copy-start.2) | copy-done | bytes 524312
  5.1 0.0 copy-start.3
  5.1 0.7 copy-done.3
  5.7 0.0 copy-start.4
  5.7 0.7 copy-done.4
  6.4 16.6 %weighted_blocks.1 = (f32[128,8,512]{2,1,0:T(8,128)S(1)}, f32[128,8,512]{2,1,0:T(8,128)}) custom-call(s32[3]{0:T(128)S(1)} %pad_add_fusion.where_ref, s32[128]{0:T(128)S(1)} %copy-done.4, s32[2,128]{1,0:T(2,128)S(1)} %bitcast.35, bf16[896,1792]{1,0:T(8,128)(2,1)S(1)} %bitcast.34, bf16[1024,1792]{1,0:T(8,128)(2,1)S(1)} %copy-done, bf16[1024,256]{1,0:T(8,128)(2,1)S(1)} %copy-done.2), custom_call_target="tpu_custom_call" | custom-call | flops 5167382528 | bytes 11075584 | tf_op jit(solution)/shard_map/weighted_blocks/pallas_call | solution.py:106
  23.1 0.1 collective-permute-start
  23.2 4.4 %collective-permute-done = f32[128,8,512]{2,1,0:T(8,128)} collective-permute-done((f32[128,8,512]{2,1,0:T(8,128)}, f32[128,8,512]{2,1,0:T(8,128)}, u32[]{:S(2)}, u32[]{:S(2)}) %collective-permute-start) | collective-permute-done | bytes 2097184 | tf_op jit(solution)/shard_map/ppermute | solution.py:166
  27.6 2.1 %add.100 = f32[128,8,512]{2,1,0:T(8,128)S(1)} add(f32[128,8,512]{2,1,0:T(8,128)S(1)} %get-tuple-element.7, f32[128,8,512]{2,1,0:T(8,128)} %collective-permute-done) | non-fusion elementwise | flops 524288 | bytes 6291456 | tf_op jit(solution)/shard_map/add | solution.py:166
  29.7 0.0 copy-start.5
  29.7 1.3 %copy-done.5 = f32[128,8,512]{2,1,0:T(8,128)} copy-done((f32[128,8,512]{2,1,0:T(8,128)}, f32[128,8,512]{2,1,0:T(8,128)S(1)}, u32[]{:S(2)}) %copy-start.5) | copy-done | bytes 2097176
  31.0 0.1 dynamic-slice_bitcast_fusion.2
  31.2 2.2 %collective-permute-start.3 = (f32[32,8,512]{2,1,0:T(8,128)S(1)}, f32[32,8,512]{2,1,0:T(8,128)S(1)}, u32[]{:S(2)}, u32[]{:S(2)}) collective-permute-start(f32[32,8,512]{2,1,0:T(8,128)S(1)} %get-tuple-element.10), channel_id=1, source_target_pairs={{0,128},{2,10},{16,144},{18,26},{32,160},{34,42},{48,176},{50,58},... | collective-permute-start | bytes 1572872 | tf_op jit(solution)/shard_map/ppermute | solution.py:158
  33.4 1.4 %collective-permute-start.2 = (f32[32,8,512]{2,1,0:T(8,128)S(1)}, f32[32,8,512]{2,1,0:T(8,128)S(1)}, u32[]{:S(2)}, u32[]{:S(2)}) collective-permute-start(f32[32,8,512]{2,1,0:T(8,128)S(1)} %get-tuple-element.11), channel_id=1, source_target_pairs={{0,129},{2,14},{16,145},{18,30},{32,161},{34,46},{48,177},{50,62},... | collective-permute-start | bytes 1572872 | tf_op jit(solution)/shard_map/ppermute | solution.py:158
  34.8 0.6 collective-permute-start.1
  35.4 6.6 %collective-permute-done.3 = f32[32,8,512]{2,1,0:T(8,128)S(1)} collective-permute-done((f32[32,8,512]{2,1,0:T(8,128)S(1)}, f32[32,8,512]{2,1,0:T(8,128)S(1)}, u32[]{:S(2)}, u32[]{:S(2)}) %collective-permute-start.3) | collective-permute-done | bytes 524320 | tf_op jit(solution)/shard_map/ppermute | solution.py:158
  42.0 5.5 %collective-permute-done.2 = f32[32,8,512]{2,1,0:T(8,128)S(1)} collective-permute-done((f32[32,8,512]{2,1,0:T(8,128)S(1)}, f32[32,8,512]{2,1,0:T(8,128)S(1)}, u32[]{:S(2)}, u32[]{:S(2)}) %collective-permute-start.2) | collective-permute-done | bytes 524320 | tf_op jit(solution)/shard_map/ppermute | solution.py:158
  47.6 0.1 collective-permute-done.1
  47.6 1.3 %fusion.1 = f32[32,8,512]{2,1,0:T(8,128)S(1)} fusion(f32[32,8,512]{2,1,0:T(8,128)S(1)} %collective-permute-done.3, f32[32,8,512]{2,1,0:T(8,128)S(1)} %collective-permute-done.2, f32[32,8,512]{2,1,0:T(8,128)S(1)} %collective-permute-done.1, f32[4,32,8,512]{3,2,1,0:T(8,128)} %bitcast.37, s32[]{:T(128)S(6)} %select_n.60), kind=kLoop, calls=%fused_computation.2 | loop fusion | flops 393216 | bytes 2621444 | tf_op jit(solution)/shard_map/add | solution.py:158
  48.9 3.3 %collective-permute-start.6 = (f32[8,8,512]{2,1,0:T(8,128)S(1)}, f32[8,8,512]{2,1,0:T(8,128)S(1)}, u32[]{:S(2)}, u32[]{:S(2)}) collective-permute-start(f32[8,8,512]{2,1,0:T(8,128)S(1)} %get-tuple-element.13), channel_id=1, source_target_pairs={{0,8},{2,130},{16,24},{18,146},{32,40},{34,162},{48,56},{50,178},{... | collective-permute-start | bytes 393224 | tf_op jit(solution)/shard_map/ppermute | solution.py:158
  52.2 1.1 %collective-permute-start.5 = (f32[8,8,512]{2,1,0:T(8,128)S(1)}, f32[8,8,512]{2,1,0:T(8,128)S(1)}, u32[]{:S(2)}, u32[]{:S(2)}) collective-permute-start(f32[8,8,512]{2,1,0:T(8,128)S(1)} %get-tuple-element.14), channel_id=1, source_target_pairs={{0,12},{2,131},{16,28},{18,147},{32,44},{34,163},{48,60},{50,179},... | collective-permute-start | bytes 393224 | tf_op jit(solution)/shard_map/ppermute | solution.py:158
  53.3 1.0 %collective-permute-start.4 = (f32[8,8,512]{2,1,0:T(8,128)S(1)}, f32[8,8,512]{2,1,0:T(8,128)S(1)}, u32[]{:S(2)}, u32[]{:S(2)}) collective-permute-start(f32[8,8,512]{2,1,0:T(8,128)S(1)} %get-tuple-element.12), channel_id=1, source_target_pairs={{0,4},{2,3},{16,20},{18,19},{32,36},{34,35},{48,52},{50,51},{64,68... | collective-permute-start | bytes 393224 | tf_op jit(solution)/shard_map/ppermute | solution.py:158
  54.2 1.2 %collective-permute-done.6 = f32[8,8,512]{2,1,0:T(8,128)S(1)} collective-permute-done((f32[8,8,512]{2,1,0:T(8,128)S(1)}, f32[8,8,512]{2,1,0:T(8,128)S(1)}, u32[]{:S(2)}, u32[]{:S(2)}) %collective-permute-start.6) | collective-permute-done | bytes 131104 | tf_op jit(solution)/shard_map/ppermute | solution.py:158
  55.5 1.7 %collective-permute-done.5 = f32[8,8,512]{2,1,0:T(8,128)S(1)} collective-permute-done((f32[8,8,512]{2,1,0:T(8,128)S(1)}, f32[8,8,512]{2,1,0:T(8,128)S(1)}, u32[]{:S(2)}, u32[]{:S(2)}) %collective-permute-start.5) | collective-permute-done | bytes 131104 | tf_op jit(solution)/shard_map/ppermute | solution.py:158
  57.2 2.2 %collective-permute-done.4 = f32[8,8,512]{2,1,0:T(8,128)S(1)} collective-permute-done((f32[8,8,512]{2,1,0:T(8,128)S(1)}, f32[8,8,512]{2,1,0:T(8,128)S(1)}, u32[]{:S(2)}, u32[]{:S(2)}) %collective-permute-start.4) | collective-permute-done | bytes 131104 | tf_op jit(solution)/shard_map/ppermute | solution.py:158
  59.5 17.3 %all_to_all.5 = f32[8,8,512]{2,1,0:T(8,128)S(1)} all-to-all(f32[8,8,512]{2,1,0:T(8,128)S(1)} %fusion.3), channel_id=1, replica_groups=mesh['xh'=2,'z'=8,'y'=4,'core'=2,'xl'=2] {'z'}, dimensions={0} | all-to-all | bytes 262144 | tf_op jit(solution)/shard_map/all_to_all | solution.py:171
  76.8 0.6 reduce_sum.9
  (2 shorter events, 0.1 us)
Async XLA Ops:
  0.1 2.0 %copy-start = (bf16[1024,1792]{1,0:T(8,128)(2,1)S(1)}, bf16[1024,1792]{1,0:T(8,128)(2,1)}, u32[]{:S(2)}) copy-start(bf16[1024,1792]{1,0:T(8,128)(2,1)} %vir_hbm.1) | copy-start | bytes 11010052
  2.1 1.9 %copy-start.1 = (bf16[1,896,1792]{2,1,0:T(8,128)(2,1)S(1)}, bf16[1,896,1792]{2,1,0:T(8,128)(2,1)}, u32[]{:S(2)}) copy-start(bf16[1,896,1792]{2,1,0:T(8,128)(2,1)} %param.5) | copy-start | bytes 9633796
  4.0 1.0 %copy-start.2 = (bf16[1024,256]{1,0:T(8,128)(2,1)S(1)}, bf16[1024,256]{1,0:T(8,128)(2,1)}, u32[]{:S(2)}) copy-start(bf16[1024,256]{1,0:T(8,128)(2,1)} %occ_ref.1) | copy-start | bytes 1572868
  5.1 0.7 copy-start.3
  5.7 0.7 copy-start.4
  23.1 4.6 %collective-permute-start = (f32[128,8,512]{2,1,0:T(8,128)}, f32[128,8,512]{2,1,0:T(8,128)}, u32[]{:S(2)}, u32[]{:S(2)}) collective-permute-start(f32[128,8,512]{2,1,0:T(8,128)} %get-tuple-element.8), channel_id=1, source_target_pairs={{0,2},{2,0},{1,3},{3,1},{4,6},{6,4},{5,7},{7,5},{8,10},{10,8},{9,1... | collective-permute-start | bytes 6291464 | tf_op jit(solution)/shard_map/ppermute | solution.py:166
  29.7 1.3 %copy-start.5 = (f32[128,8,512]{2,1,0:T(8,128)}, f32[128,8,512]{2,1,0:T(8,128)S(1)}, u32[]{:S(2)}) copy-start(f32[128,8,512]{2,1,0:T(8,128)S(1)} %add.100) | copy-start | bytes 6291460
  31.2 10.9 %collective-permute-start.3 = (f32[32,8,512]{2,1,0:T(8,128)S(1)}, f32[32,8,512]{2,1,0:T(8,128)S(1)}, u32[]{:S(2)}, u32[]{:S(2)}) collective-permute-start(f32[32,8,512]{2,1,0:T(8,128)S(1)} %get-tuple-element.10), channel_id=1, source_target_pairs={{0,128},{2,10},{16,144},{18,26},{32,160},{34,42},{48,176},{50,58},... | collective-permute-start | bytes 1572872 | tf_op jit(solution)/shard_map/ppermute | solution.py:158
  33.4 14.2 %collective-permute-start.2 = (f32[32,8,512]{2,1,0:T(8,128)S(1)}, f32[32,8,512]{2,1,0:T(8,128)S(1)}, u32[]{:S(2)}, u32[]{:S(2)}) collective-permute-start(f32[32,8,512]{2,1,0:T(8,128)S(1)} %get-tuple-element.11), channel_id=1, source_target_pairs={{0,129},{2,14},{16,145},{18,30},{32,161},{34,46},{48,177},{50,62},... | collective-permute-start | bytes 1572872 | tf_op jit(solution)/shard_map/ppermute | solution.py:158
  34.8 12.8 %collective-permute-start.1 = (f32[32,8,512]{2,1,0:T(8,128)S(1)}, f32[32,8,512]{2,1,0:T(8,128)S(1)}, u32[]{:S(2)}, u32[]{:S(2)}) collective-permute-start(f32[32,8,512]{2,1,0:T(8,128)S(1)} %get-tuple-element.9), channel_id=1, source_target_pairs={{0,1},{2,6},{16,17},{18,22},{32,33},{34,38},{48,49},{50,54},{64,65... | collective-permute-start | bytes 1572872 | tf_op jit(solution)/shard_map/ppermute | solution.py:158
  48.9 6.6 %collective-permute-start.6 = (f32[8,8,512]{2,1,0:T(8,128)S(1)}, f32[8,8,512]{2,1,0:T(8,128)S(1)}, u32[]{:S(2)}, u32[]{:S(2)}) collective-permute-start(f32[8,8,512]{2,1,0:T(8,128)S(1)} %get-tuple-element.13), channel_id=1, source_target_pairs={{0,8},{2,130},{16,24},{18,146},{32,40},{34,162},{48,56},{50,178},{... | collective-permute-start | bytes 393224 | tf_op jit(solution)/shard_map/ppermute | solution.py:158
  52.2 5.0 %collective-permute-start.5 = (f32[8,8,512]{2,1,0:T(8,128)S(1)}, f32[8,8,512]{2,1,0:T(8,128)S(1)}, u32[]{:S(2)}, u32[]{:S(2)}) collective-permute-start(f32[8,8,512]{2,1,0:T(8,128)S(1)} %get-tuple-element.14), channel_id=1, source_target_pairs={{0,12},{2,131},{16,28},{18,147},{32,44},{34,163},{48,60},{50,179},... | collective-permute-start | bytes 393224 | tf_op jit(solution)/shard_map/ppermute | solution.py:158
  53.3 6.2 %collective-permute-start.4 = (f32[8,8,512]{2,1,0:T(8,128)S(1)}, f32[8,8,512]{2,1,0:T(8,128)S(1)}, u32[]{:S(2)}, u32[]{:S(2)}) collective-permute-start(f32[8,8,512]{2,1,0:T(8,128)S(1)} %get-tuple-element.12), channel_id=1, source_target_pairs={{0,4},{2,3},{16,20},{18,19},{32,36},{34,35},{48,52},{50,51},{64,68... | collective-permute-start | bytes 393224 | tf_op jit(solution)/shard_map/ppermute | solution.py:158
